TPU v7x, 32 devices: a whole 2x2x4 slice. The times are simulated.
32 devices in a mesh: grp: 4 (over x, core), seq: 8 (over z, y).
Axes of the slice: x: 2, y: 2, z: 4, core: 2. Of those that a mesh axis runs over, the one named last changes fastest.
Arguments:
- patches: bfloat16 [2048, 1280], P(('grp', 'seq')), may hold values from -60 to 60
- piece_ids: int32 [32, 64], P(('grp', 'seq')), may hold values from 0 to 2, never falling along the last dimension, each value on 1 to 48 neighbouring positions
- vit_gain: float32 [1280], replicated, may hold values from 0.25 to 1.75
- vit_qkv: bfloat16 [1280, 3840], replicated
- vit_out: bfloat16 [1280, 1280], replicated, may hold values from -0.15625 to 0.15625
- merge_gain: float32 [1280], replicated, may hold values from 0.25 to 1.75
- merge_up: bfloat16 [5120, 5120], P(None, 'seq'), may hold values from -0.078125 to 0.078125
- merge_down: bfloat16 [5120, 8192], P(None, 'seq'), may hold values from -0.078125 to 0.078125
- dest: int32 [512], P(('grp', 'seq')), may hold values from 0 to 7, as said below
- tokens: bfloat16 [8192, 8192], P(('grp', 'seq')), may hold values from -60 to 60
- image_index: int32 [8192], P(('grp', 'seq')), may hold values from 0 to 32, as said below
- doc_lengths: int32 [4, 4], P('grp'), may hold values from 1 to 1024, 2048 in all within a row
- attn_gain: float32 [8192], replicated, may hold values from 0.25 to 1.75
- attn_qkv: bfloat16 [8192, 768], P(('grp', 'seq'))
- attn_out: bfloat16 [512, 8192], P(None, ('grp', 'seq')), may hold values from -0.25 to 0.25
Outputs:
- layer_out: bfloat16 [8192, 8192], P(('grp', 'seq'))
Inputs may be any that keep to these rules, and one draw needn't show every extreme that they name: `dest`: within each aligned block of 16 rows (one device's merged rows), exactly 4 distinct values occur, each exactly 4 times, and in every group one device is named by every device of the group. `image_index`: 32 marks a text token. A value k < 32 on a device names the merged row that the device of seq index k // 4 in its group sends to it as its (k % 4)-th row in row order; each such row is named by exactly one token of the receiving device, and no other values occur. `piece_ids`: piece numbers never fall within a window. `doc_lengths`: each group's documents fill its 2048 positions.
All inputs are finite; a program needn't handle non-finite values.
Results may differ from a plain program's by a relative error of at most 0.0093.
The roundings to bfloat16 on the way count: a program that leaves them out, or rounds other values in their place, can miss the bound.
Values may be sent and summed in bfloat16 or wider, within the bound.
A program may use at most 192 MiB of HBM per device.

v0:
```python
import jax
import jax.numpy as jnp
from jax import lax
from jax.sharding import PartitionSpec as P

VHEADS = 16
WIN = 64
EPSILON = 1e-06


def from_behind(value, axis, steps):
    count = lax.axis_size(axis)
    first, last = (max(0, -steps), min(count, count - steps))
    return lax.ppermute(value, axis, [(source, source + steps) for source in range(first, last)])


def rms_scale(inputs, gain):
    mean_square = jnp.mean(inputs * inputs, axis=-1, keepdims=True)
    return inputs * lax.rsqrt(mean_square + EPSILON) * gain


def softmax_mix(scores, allowed, value_collection, spec):
    scores = jnp.where(allowed[None], scores, -1e30)
    highest = jnp.max(scores, axis=-1, keepdims=True)
    weights = jnp.exp(scores - highest)
    totals = jnp.sum(weights, axis=-1)
    mixture = jnp.einsum(
        spec, weights.astype(jnp.bfloat16), value_collection, preferred_element_type=jnp.float32
    )
    return mixture / jnp.transpose(totals)[:, :, None]


def window_layer(patch_rows, piece_rows, vit_gain, vit_qkv, vit_out, merge_gain):
    row_count, features = patch_rows.shape
    head_dim = features // VHEADS
    residual = patch_rows.astype(jnp.float32)
    normed = rms_scale(residual, vit_gain).astype(jnp.bfloat16)
    projected = jnp.dot(normed, vit_qkv, preferred_element_type=jnp.float32).astype(jnp.bfloat16)
    queries = projected[:, :features].reshape(row_count, VHEADS, head_dim)
    key_set = projected[:, features : 2 * features].reshape(row_count, VHEADS, head_dim)
    value_collection = projected[:, 2 * features :].reshape(row_count, VHEADS, head_dim)
    scores = jnp.einsum(
        "qhd,khd->hqk", queries, key_set, preferred_element_type=jnp.float32
    ) * head_dim ** (-0.5)
    frames = jnp.arange(row_count, dtype=jnp.int32) // WIN
    allowed = (frames[:, None] == frames[None, :]) & (piece_rows[:, None] == piece_rows[None, :])
    mixture = softmax_mix(scores, allowed, value_collection, "hqk,khd->qhd")
    mixture = mixture.reshape(row_count, features).astype(jnp.bfloat16)
    residual = residual + jnp.dot(mixture, vit_out, preferred_element_type=jnp.float32)
    merge_input = rms_scale(residual, merge_gain).astype(jnp.bfloat16)
    return merge_input.reshape(row_count // 4, 4 * features)


def attend(query_rows, query_pos, query_start, key_value, key_pos):
    row_count = query_rows.shape[0]
    head_dim = key_value.shape[1] // 2
    heads = query_rows.shape[1] // head_dim
    queries = query_rows.reshape(row_count, heads, head_dim)
    scores = jnp.einsum(
        "qhd,kd->hqk", queries, key_value[:, :head_dim], preferred_element_type=jnp.float32
    ) * head_dim ** (-0.5)
    allowed = (key_pos[None, :] >= query_start[:, None]) & (key_pos[None, :] <= query_pos[:, None])
    mixture = softmax_mix(scores, allowed, key_value[:, head_dim:], "hqk,kd->qhd")
    return mixture.reshape(row_count, heads * head_dim).astype(jnp.bfloat16)


def slot_numbers(targets):
    row_count = targets.shape[-1]
    order = jnp.arange(row_count, dtype=jnp.int32)
    same = targets[..., :, None] == targets[..., None, :]
    earlier = order[None, :] < order[:, None]
    return jnp.sum(same & earlier, axis=-1)


def on_device(
    patches,
    piece_ids,
    vit_gain,
    vit_qkv,
    vit_out,
    merge_gain,
    merge_up,
    merge_down,
    dest,
    tokens,
    image_index,
    doc_lengths,
    attn_gain,
    attn_qkv,
    attn_out,
):
    features = patches.shape[1]
    block_len = WIN
    patch_blocks = patches.reshape(-1, block_len, features)
    merge_input = lax.map(
        lambda parts: window_layer(parts[0], parts[1], vit_gain, vit_qkv, vit_out, merge_gain),
        (patch_blocks, piece_ids),
    ).reshape(-1, 4 * features)
    own_rows = merge_input.shape[0]
    seq_count = lax.axis_size("seq")
    seq_index = lax.axis_index("seq")
    hidden_part = jax.nn.gelu(
        jnp.dot(
            lax.all_gather(merge_input, "seq", axis=0, tiled=True),
            merge_up,
            preferred_element_type=jnp.float32,
        ),
        approximate=False,
    ).astype(jnp.bfloat16)
    column_part = jnp.dot(
        lax.all_gather(hidden_part, "seq", axis=1, tiled=True),
        merge_down,
        preferred_element_type=jnp.float32,
    ).astype(jnp.bfloat16)
    capacity = own_rows // (seq_count // 2)
    slots = seq_count * capacity
    receivers = jnp.arange(seq_count, dtype=jnp.int32)
    slot_ids = jnp.arange(capacity, dtype=jnp.int32)
    home_rows = lax.all_to_all(column_part, "seq", split_axis=0, concat_axis=1, tiled=True)
    order = slot_numbers(dest)
    select = (dest[None, None, :] == receivers[:, None, None]) & (
        order[None, None, :] == slot_ids[None, :, None]
    )
    outgoing = jnp.einsum(
        "dcj,jf->dcf", select.astype(jnp.bfloat16), home_rows, preferred_element_type=jnp.float32
    ).astype(jnp.bfloat16)
    arrived = lax.all_to_all(outgoing, "seq", split_axis=0, concat_axis=0, tiled=True).reshape(
        slots, -1
    )
    slot_all = jnp.arange(slots, dtype=jnp.int32)
    picker = (image_index[:, None] == slot_all[None, :]).astype(jnp.bfloat16)
    pictured = jnp.dot(picker, arrived, preferred_element_type=jnp.float32).astype(jnp.bfloat16)
    layer_in = jnp.where((image_index < slots)[:, None], pictured, tokens)
    tok_rows = tokens.shape[0]
    normed = rms_scale(layer_in.astype(jnp.float32), attn_gain).astype(jnp.bfloat16)
    projected = jnp.dot(
        normed,
        lax.all_gather(attn_qkv, ("grp", "seq"), axis=0, tiled=True),
        preferred_element_type=jnp.float32,
    ).astype(jnp.bfloat16)
    query_width = attn_out.shape[0]
    queries = projected[:, :query_width]
    key_value = projected[:, query_width:]
    head_dim = key_value.shape[1] // 2
    head_count = query_width // head_dim
    positions = seq_index * tok_rows + jnp.arange(tok_rows, dtype=jnp.int32)
    lengths = doc_lengths[0]
    starts = jnp.cumsum(lengths) - lengths
    doc_start = jnp.max(
        jnp.where(starts[None, :] <= positions[:, None], starts[None, :], 0), axis=1
    )
    reach = seq_count // 2
    buffer = jnp.zeros(((reach + 1) * tok_rows, key_value.shape[1]), key_value.dtype)
    buffer = lax.dynamic_update_slice_in_dim(buffer, key_value, reach * tok_rows, 0)

    def step_back(turn, state):
        current, filled = state
        current = from_behind(current, "seq", 1)
        filled = lax.dynamic_update_slice_in_dim(filled, current, (reach - turn) * tok_rows, 0)
        return (current, filled)

    key_rows = lax.fori_loop(1, reach + 1, step_back, (key_value, buffer))[1]
    key_pos = (seq_index - reach) * tok_rows + jnp.arange(key_rows.shape[0], dtype=jnp.int32)
    block_rows = min(tok_rows, 512)
    head_queries = queries.reshape(tok_rows, head_count, head_dim).transpose(1, 0, 2)

    def one_head(head_rows):
        return lax.map(
            lambda parts: attend(parts[0], parts[1], parts[2], key_rows, key_pos),
            (
                head_rows.reshape(-1, block_rows, head_dim),
                positions.reshape(-1, block_rows),
                doc_start.reshape(-1, block_rows),
            ),
        ).reshape(tok_rows, head_dim)

    attended = lax.map(one_head, head_queries).transpose(1, 0, 2).reshape(tok_rows, query_width)
    update = jnp.dot(
        attended,
        lax.all_gather(attn_out, ("grp", "seq"), axis=1, tiled=True),
        preferred_element_type=jnp.float32,
    )
    return (layer_in.astype(jnp.float32) + update).astype(jnp.bfloat16)


def solution(mesh):
    placed = (
        P(("grp", "seq"), None),
        P(("grp", "seq"), None),
        P(),
        P(),
        P(),
        P(),
        P(None, "seq"),
        P(None, "seq"),
        P(("grp", "seq")),
        P(("grp", "seq"), None),
        P(("grp", "seq")),
        P("grp", None),
        P(),
        P(("grp", "seq"), None),
        P(None, ("grp", "seq")),
    )
    return jax.shard_map(
        on_device, mesh=mesh, in_specs=placed, out_specs=P(("grp", "seq"), None), check_vma=False
    )
```

profile of v0, /device:TPU:0, one launch (start us, length us, event | category | flops | bytes accessed | tf_op | source)
XLA Modules:
  0.0 336.6 jit_solution(14184736836307715326)
XLA Ops:
  7.8 5.8 %convolution_convert_fusion.2 = bf16[64,3840]{1,0:T(8,128)(2,1)S(1)} fusion(bf16[1280,3840]{1,0:T(8,128)(2,1)} %param.22, bf16[64,1280]{1,0:T(8,128)(2,1)} %param.19, f32[1280]{0:T(1024)} %param.21, f32[64]{0:T(128)S(1)} %add_rsqrt_fusion.2), kind=kOutput, calls=%fused_computation.33 | convolution fusion | flops 629719040 | bytes 10491136 | tf_op jit(solution)/shard_map/while/body/eval_jaxpr/dot_general | solution.py:38
  28.7 44.6 %all-gather.5.cloned.1.call-done = bf16[128,5120]{1,0:T(8,128)(2,1)} async-done(((bf16[16,5120]{1,0:T(8,128)(2,1)}), bf16[128,5120]{1,0:T(8,128)(2,1)}) %all-gather.5.cloned.1.call-update) | async-done | bytes 1310736 | tf_op jit(solution)/shard_map/all_gather | solution.py:104
  73.3 5.8 %fusion.41 = bf16[128,640]{1,0:T(8,128)(2,1)} fusion(bf16[128,5120]{1,0:T(8,128)(2,1)} %all-gather.5.cloned.1.call-done, bf16[5120,640]{1,0:T(8,128)(2,1)} %param.25), kind=kOutput, calls=%fused_computation.56 | convolution fusion | flops 844185600 | bytes 8028160 | tf_op jit(solution)/shard_map/dot_general | solution.py:103
  80.4 40.2 %all-gather.7.cloned.1.call-done = bf16[128,5120]{1,0:T(8,128)(2,1)} async-done(((bf16[128,640]{1,0:T(8,128)(2,1)}), bf16[128,5120]{1,0:T(8,128)(2,1)}) %all-gather.7.cloned.1.call-update) | async-done | bytes 1310736 | tf_op jit(solution)/shard_map/all_gather | solution.py:111
  120.6 6.6 %convolution_convert_fusion.3 = bf16[128,1024]{1,0:T(8,128)(2,1)} fusion(bf16[128,5120]{1,0:T(8,128)(2,1)} %all-gather.7.cloned.1.call-done, bf16[5120,1024]{1,0:T(8,128)(2,1)} %param.26), kind=kOutput, calls=%fused_computation.44 | convolution fusion | flops 1342308352 | bytes 12058624 | tf_op jit(solution)/shard_map/dot_general | solution.py:110
  127.3 3.5 %all-to-all-start = ((bf16[8,16,1024]{2,1,0:T(8,128)(2,1)}), bf16[8,16,1024]{2,1,0:T(8,128)(2,1)S(1)}, u32[]{:S(2)}, u32[]{:S(2)}) async-start(bf16[8,16,1024]{2,1,0:T(8,128)(2,1)} %bitcast.3), calls=%async_computation | async-start | bytes 524288 | tf_op jit(solution)/shard_map/all_to_all | solution.py:119
  131.0 13.7 %all-to-all-done = bf16[8,16,1024]{2,1,0:T(8,128)(2,1)S(1)} async-done(((bf16[8,16,1024]{2,1,0:T(8,128)(2,1)}), bf16[8,16,1024]{2,1,0:T(8,128)(2,1)S(1)}, u32[]{:S(2)}, u32[]{:S(2)}) %all-to-all-start) | async-done | bytes 262176 | tf_op jit(solution)/shard_map/all_to_all | solution.py:119
  146.5 3.7 %all-to-all-start.1 = ((bf16[8,4,8192]{2,1,0:T(4,128)(2,1)}), bf16[8,4,8192]{2,1,0:T(4,128)(2,1)S(1)}, u32[]{:S(2)}, u32[]{:S(2)}) async-start(bf16[8,4,8192]{2,1,0:T(4,128)(2,1)} %copy.46), calls=%async_computation.1 | async-start | bytes 1048576 | tf_op jit(solution)/shard_map/all_to_all | solution.py:127
  150.4 25.3 %all-to-all-done.1 = bf16[8,4,8192]{2,1,0:T(4,128)(2,1)S(1)} async-done(((bf16[8,4,8192]{2,1,0:T(4,128)(2,1)}), bf16[8,4,8192]{2,1,0:T(4,128)(2,1)S(1)}, u32[]{:S(2)}, u32[]{:S(2)}) %all-to-all-start.1) | async-done | bytes 524320 | tf_op jit(solution)/shard_map/all_to_all | solution.py:127
  175.9 4.8 %fusion.21 = (f32[256]{0:T(256)S(1)}, bf16[256,8192]{1,0:T(8,128)(2,1)}) fusion(bf16[256,8192]{1,0:T(8,128)(2,1)} %param.28, bf16[32,8192]{1,0:T(8,128)(2,1)S(1)} %reshape.349, s32[256]{0:T(256)S(1)} %copy-done.6, pred[256]{0:T(512)(128)(4,1)S(1)} %broadcast_compare_fusion), kind=kOutput, calls=%fused_computation.30 | convolution fusion | flops 144711424 | bytes 8915200 | tf_op jit(solution)/shard_map/dot_general | solution.py:132
  180.7 44.7 %all-gather.9.cloned.1.call-done = bf16[8192,768]{1,0:T(8,128)(2,1)} async-done(((bf16[256,768]{1,0:T(8,128)(2,1)}), bf16[8192,768]{1,0:T(8,128)(2,1)}) %all-gather.9.cloned.1.call-update) | async-done | bytes 12582928 | tf_op jit(solution)/shard_map/all_gather | solution.py:138
  225.4 9.3 %fusion.28 = bf16[256,768]{1,0:T(8,128)(2,1)S(1)} fusion(bf16[8192,768]{1,0:T(8,128)(2,1)} %all-gather.9.cloned.1.call-done, bf16[256,8192]{1,0:T(8,128)(2,1)} %get-tuple-element.202, f32[8192]{0:T(1024)S(1)} %copy-done.5, f32[256]{0:T(256)S(1)} %add_rsqrt_fusion), kind=kOutput, calls=%fused_computation.38 | convolution fusion | flops 3229810688 | bytes 17204224 | tf_op jit(solution)/shard_map/dot_general | solution.py:136
  234.9 30.8 %while.20 = (s32[]{:T(128)}, bf16[256,256]{1,0:T(8,128)(2,1)S(1)}, bf16[1280,256]{1,0:T(8,128)(2,1)S(1)}, s32[]{:T(128)}, s32[]{:T(128)}, /*index=5*/s32[]{:T(128)}, s32[]{:T(128)}, s32[]{:T(128)}) while((s32[]{:T(128)}, bf16[256,256]{1,0:T(8,128)(2,1)S(1)}, bf16[1280,256]{1,0:T(8,128)(2,1)S(1)}, s32[]{:T(128)}, s32[]{:T(128)}, ...), condition=%wide.region_9.10_spmd, body=%wide.region_8.9_spmd.sunk | while | flops 7 | bytes 1048763 | solution.py:162
  234.9 3.4 %collective-permute-start = (bf16[256,256]{1,0:T(8,128)(2,1)S(1)}, bf16[256,256]{1,0:T(8,128)(2,1)S(1)}, u32[]{:S(2)}, u32[]{:S(2)}) collective-permute-start(bf16[256,256]{1,0:T(8,128)(2,1)S(1)} %get-tuple-element.278), channel_id=1, source_target_pairs={{0,1},{1,2},{2,3},{3,4},{4,5},{5,6},{6,7},{8,9},{9,10},{10,11},{11... | collective-permute-start | bytes 393224 | tf_op jit(solution)/shard_map/while/body/eval_jaxpr/ppermute | solution.py:14
  238.3 3.1 collective-permute-done
  241.5 4.4 %collective-permute-start = (bf16[256,256]{1,0:T(8,128)(2,1)S(1)}, bf16[256,256]{1,0:T(8,128)(2,1)S(1)}, u32[]{:S(2)}, u32[]{:S(2)}) collective-permute-start(bf16[256,256]{1,0:T(8,128)(2,1)S(1)} %get-tuple-element.278), channel_id=1, source_target_pairs={{0,1},{1,2},{2,3},{3,4},{4,5},{5,6},{6,7},{8,9},{9,10},{10,11},{11... | collective-permute-start | bytes 393224 | tf_op jit(solution)/shard_map/while/body/eval_jaxpr/ppermute | solution.py:14
  245.9 2.5 collective-permute-done
  248.4 4.5 %collective-permute-start = (bf16[256,256]{1,0:T(8,128)(2,1)S(1)}, bf16[256,256]{1,0:T(8,128)(2,1)S(1)}, u32[]{:S(2)}, u32[]{:S(2)}) collective-permute-start(bf16[256,256]{1,0:T(8,128)(2,1)S(1)} %get-tuple-element.278), channel_id=1, source_target_pairs={{0,1},{1,2},{2,3},{3,4},{4,5},{5,6},{6,7},{8,9},{9,10},{10,11},{11... | collective-permute-start | bytes 393224 | tf_op jit(solution)/shard_map/while/body/eval_jaxpr/ppermute | solution.py:14
  252.9 4.7 %collective-permute-done = bf16[256,256]{1,0:T(8,128)(2,1)S(1)} collective-permute-done((bf16[256,256]{1,0:T(8,128)(2,1)S(1)}, bf16[256,256]{1,0:T(8,128)(2,1)S(1)}, u32[]{:S(2)}, u32[]{:S(2)}) %collective-permute-start) | collective-permute-done | bytes 131104 | tf_op jit(solution)/shard_map/while/body/eval_jaxpr/ppermute | solution.py:14
  257.7 5.5 %collective-permute-start = (bf16[256,256]{1,0:T(8,128)(2,1)S(1)}, bf16[256,256]{1,0:T(8,128)(2,1)S(1)}, u32[]{:S(2)}, u32[]{:S(2)}) collective-permute-start(bf16[256,256]{1,0:T(8,128)(2,1)S(1)} %get-tuple-element.278), channel_id=1, source_target_pairs={{0,1},{1,2},{2,3},{3,4},{4,5},{5,6},{6,7},{8,9},{9,10},{10,11},{11... | collective-permute-start | bytes 393224 | tf_op jit(solution)/shard_map/while/body/eval_jaxpr/ppermute | solution.py:14
  263.2 2.5 collective-permute-done
  265.7 5.9 %while.21 = (s32[]{:T(128)}, bf16[4,256,128]{1,2,0:T(8,128)(2,1)S(1)}, s32[256]{0:T(256)S(1)}, bf16[4,256,128]{2,1,0:T(8,128)(2,1)S(1)}, bf16[1280,256]{1,0:T(8,...) while((s32[]{:T(128)}, bf16[4,256,128]{1,2,0:T(8,128)(2,1)S(1)}, s32[256]{0:T(256)S(1)}, ...), condition=%wide.region_13.14_spmd.clone, body=%wide.region_10.13_spmd.clone.sunk | while | flops 171115520 | bytes 5002341 | solution.py:177
  271.6 49.3 %all-gather.11.cloned.1.call-done = bf16[512,8192]{1,0:T(8,128)(2,1)} async-done(((bf16[512,256]{1,0:T(8,128)(2,1)}), bf16[512,8192]{1,0:T(8,128)(2,1)}) %all-gather.11.cloned.1.call-update) | async-done | bytes 8388624 | tf_op jit(solution)/shard_map/all_gather | solution.py:180
  320.9 9.2 %fusion.19 = bf16[256,8192]{1,0:T(8,128)(2,1)} fusion(bf16[256,512]{0,1:T(8,128)(2,1)S(1)} %bitcast.73, bf16[512,8192]{1,0:T(8,128)(2,1)} %all-gather.11.cloned.1.call-done, bf16[256,8192]{1,0:T(8,128)(2,1)} %get-tuple-element.202), kind=kOutput, calls=%fused_computation.26 | convolution fusion | flops 2153775104 | bytes 17039360 | tf_op jit(solution)/shard_map/dot_general | solution.py:178
  (97 shorter events, 25.7 us)
Async XLA Ops:
  6.5 19.4 %copy-start = (bf16[1280,1280]{1,0:T(8,128)(2,1)S(1)}, bf16[1280,1280]{1,0:T(8,128)(2,1)}, u32[]{:S(2)}) copy-start(bf16[1280,1280]{1,0:T(8,128)(2,1)} %param.23) | copy-start | bytes 9830404
  6.5 66.8 %all-gather.5.cloned.1.call-start = ((), (), s32[]{:S(2)}) async-start(), calls=%async_computation.2 | async-start | bytes 1474560 | tf_op jit(solution)/shard_map/all_gather | solution.py:104
  7.8 12.6 %copy-start.4 = (s32[1,64]{1,0:T(1,128)S(1)}, s32[1,64]{1,0:T(1,128)}, u32[]{:S(2)}) copy-start(s32[1,64]{1,0:T(1,128)} %param.20) | copy-start | bytes 772
  13.6 12.4 %copy-start.2 = (bf16[64,1280]{1,0:T(8,128)(2,1)S(1)}, bf16[64,1280]{1,0:T(8,128)(2,1)}, u32[]{:S(2)}) copy-start(bf16[64,1280]{1,0:T(8,128)(2,1)} %param.19) | copy-start | bytes 491524
  21.8 5.9 %copy-start.3 = (f32[1280]{0:T(1024)S(1)}, f32[1280]{0:T(1024)}, u32[]{:S(2)}) copy-start(f32[1280]{0:T(1024)} %param.24) | copy-start | bytes 15364
  28.6 92.0 %all-gather.7.cloned.1.call-start = ((), (), s32[]{:S(2)}) async-start(), calls=%async_computation.3 | async-start | bytes 1474560 | tf_op jit(solution)/shard_map/all_gather | solution.py:111
  79.1 146.3 %all-gather.9.cloned.1.call-start = ((), (), s32[]{:S(2)}) async-start(), calls=%async_computation.4 | async-start | bytes 12976128 | tf_op jit(solution)/shard_map/all_gather | solution.py:138
  79.8 241.0 %all-gather.11.cloned.1.call-start = ((), (), s32[]{:S(2)}) async-start(), calls=%async_computation.5 | async-start | bytes 8650752 | tf_op jit(solution)/shard_map/all_gather | solution.py:180
  80.4 50.4 %copy-start.7 = (s32[16]{0:T(128)S(1)}, s32[16]{0:T(128)}, u32[]{:S(2)}) copy-start(s32[16]{0:T(128)} %param.27) | copy-start | bytes 196
  127.3 22.9 %copy-start.8 = (s32[1,4]{1,0:T(1,128)S(1)}, s32[1,4]{1,0:T(1,128)}, u32[]{:S(2)}) copy-start(s32[1,4]{1,0:T(1,128)} %param.30) | copy-start | bytes 52
  127.3 23.2 %copy-start.6 = (s32[256]{0:T(256)S(1)}, s32[256]{0:T(256)}, u32[]{:S(2)}) copy-start(s32[256]{0:T(256)} %param.29) | copy-start | bytes 3076
  127.3 17.4 %all-to-all-start = ((bf16[8,16,1024]{2,1,0:T(8,128)(2,1)}), bf16[8,16,1024]{2,1,0:T(8,128)(2,1)S(1)}, u32[]{:S(2)}, u32[]{:S(2)}) async-start(bf16[8,16,1024]{2,1,0:T(8,128)(2,1)} %bitcast.3), calls=%async_computation | async-start | bytes 524288 | tf_op jit(solution)/shard_map/all_to_all | solution.py:119
  146.5 29.3 %all-to-all-start.1 = ((bf16[8,4,8192]{2,1,0:T(4,128)(2,1)}), bf16[8,4,8192]{2,1,0:T(4,128)(2,1)S(1)}, u32[]{:S(2)}, u32[]{:S(2)}) async-start(bf16[8,4,8192]{2,1,0:T(4,128)(2,1)} %copy.46), calls=%async_computation.1 | async-start | bytes 1048576 | tf_op jit(solution)/shard_map/all_to_all | solution.py:127
  175.9 49.5 %copy-start.5 = (f32[8192]{0:T(1024)S(1)}, f32[8192]{0:T(1024)}, u32[]{:S(2)}) copy-start(f32[8192]{0:T(1024)} %param.31) | copy-start | bytes 98308
  234.9 6.5 %collective-permute-start = (bf16[256,256]{1,0:T(8,128)(2,1)S(1)}, bf16[256,256]{1,0:T(8,128)(2,1)S(1)}, u32[]{:S(2)}, u32[]{:S(2)}) collective-permute-start(bf16[256,256]{1,0:T(8,128)(2,1)S(1)} %get-tuple-element.278), channel_id=1, source_target_pairs={{0,1},{1,2},{2,3},{3,4},{4,5},{5,6},{6,7},{8,9},{9,10},{10,11},{11... | collective-permute-start | bytes 393224 | tf_op jit(solution)/shard_map/while/body/eval_jaxpr/ppermute | solution.py:14
  241.5 6.9 %collective-permute-start = (bf16[256,256]{1,0:T(8,128)(2,1)S(1)}, bf16[256,256]{1,0:T(8,128)(2,1)S(1)}, u32[]{:S(2)}, u32[]{:S(2)}) collective-permute-start(bf16[256,256]{1,0:T(8,128)(2,1)S(1)} %get-tuple-element.278), channel_id=1, source_target_pairs={{0,1},{1,2},{2,3},{3,4},{4,5},{5,6},{6,7},{8,9},{9,10},{10,11},{11... | collective-permute-start | bytes 393224 | tf_op jit(solution)/shard_map/while/body/eval_jaxpr/ppermute | solution.py:14
  248.4 9.2 %collective-permute-start = (bf16[256,256]{1,0:T(8,128)(2,1)S(1)}, bf16[256,256]{1,0:T(8,128)(2,1)S(1)}, u32[]{:S(2)}, u32[]{:S(2)}) collective-permute-start(bf16[256,256]{1,0:T(8,128)(2,1)S(1)} %get-tuple-element.278), channel_id=1, source_target_pairs={{0,1},{1,2},{2,3},{3,4},{4,5},{5,6},{6,7},{8,9},{9,10},{10,11},{11... | collective-permute-start | bytes 393224 | tf_op jit(solution)/shard_map/while/body/eval_jaxpr/ppermute | solution.py:14
  257.7 8.0 %collective-permute-start = (bf16[256,256]{1,0:T(8,128)(2,1)S(1)}, bf16[256,256]{1,0:T(8,128)(2,1)S(1)}, u32[]{:S(2)}, u32[]{:S(2)}) collective-permute-start(bf16[256,256]{1,0:T(8,128)(2,1)S(1)} %get-tuple-element.278), channel_id=1, source_target_pairs={{0,1},{1,2},{2,3},{3,4},{4,5},{5,6},{6,7},{8,9},{9,10},{10,11},{11... | collective-permute-start | bytes 393224 | tf_op jit(solution)/shard_map/while/body/eval_jaxpr/ppermute | solution.py:14
  320.9 9.2 %copy-start.1 = (bf16[1280,1280]{1,0:T(8,128)(2,1)S(1)}, bf16[1280,1280]{1,0:T(8,128)(2,1)}, u32[]{:S(2)}) copy-start(bf16[1280,1280]{1,0:T(8,128)(2,1)} %param.23) | copy-start | bytes 9830404
Sparse Core Ops, SparseCore 0:
  28.7 44.5 all-gather.4
  79.2 41.3 all-gather.6
  123.6 101.8 all-gather.8
  228.2 92.6 all-gather.10
where the time goes:
time: 337 us
  waiting for transfers between devices  232 us (69%)
  matrix products  49.9 us (15%)
  starting transfers between devices  25.1 us (7%)
  between operations  13.4 us (4%)
  local copies, waits for them, and re-layouts  12.6 us (4%)
  other arithmetic  3.41 us (1%)
    all_gather x1, waiting for transfers between devices, on_device(): lax.all_gather(attn_out, ('grp', 'seq'), axis=1, tiled=True)  49.3 us
    all_gather x1, waiting for transfers between devices, on_device(): lax.all_gather(attn_qkv, ('grp', 'seq'), axis=0, tiled=True)  44.7 us
    all_gather x1, waiting for transfers between devices, on_device(): lax.all_gather(merge_input, 'seq', axis=0, tiled=True)  44.6 us
    all_gather x1, waiting for transfers between devices, on_device(): lax.all_gather(hidden_part, 'seq', axis=1, tiled=True)  40.2 us
    all_to_all x1, waiting for transfers between devices, on_device(): lax.all_to_all(outgoing, 'seq', split_axis=0, concat_axis=0, tiled=True)  25.3 us
    ppermute x4, starting transfers between devices, from_behind(): lax.ppermute(value, axis, [(source, source + steps) for source in range(f...  17.7 us
    all_to_all x1, waiting for transfers between devices, on_device(): lax.all_to_all(column_part, 'seq', split_axis=0, concat_axis=1, tiled=True)  13.7 us
    ppermute x4, waiting for transfers between devices, from_behind(): lax.ppermute(value, axis, [(source, source + steps) for source in range(f...  12.8 us
  transfers between devices with their start and end apart: 10, of which 10 were waited for; matrix products, arithmetic and copies ran while one was open for 9% of the time, Pallas kernels for 0%

commit v1 on v0

--- a/solution.py
+++ b/solution.py
@@ -89,6 +89,18 @@
     attn_qkv,
     attn_out,
 ):
+
+    def connect_the_signs(s0, axis_tag, axis_no):
+        return jnp.concatenate(
+            lax.all_to_all(
+                jnp.stack([s0] * lax.axis_size(axis_tag)),
+                axis_name=axis_tag,
+                split_axis=0,
+                concat_axis=0,
+            ),
+            axis_no,
+        )
+
     features = patches.shape[1]
     block_len = WIN
     patch_blocks = patches.reshape(-1, block_len, features)
@@ -134,9 +146,7 @@
     tok_rows = tokens.shape[0]
     normed = rms_scale(layer_in.astype(jnp.float32), attn_gain).astype(jnp.bfloat16)
     projected = jnp.dot(
-        normed,
-        lax.all_gather(attn_qkv, ("grp", "seq"), axis=0, tiled=True),
-        preferred_element_type=jnp.float32,
+        normed, connect_the_signs(attn_qkv, ("grp", "seq"), 0), preferred_element_type=jnp.float32
     ).astype(jnp.bfloat16)
     query_width = attn_out.shape[0]
     queries = projected[:, :query_width]

time: 337 us -> 554 us (1.64)
  waiting for transfers between devices: 232 us -> 427 us
  blocking collectives: 0 us -> 16.9 us
    all_to_all x1, waiting for transfers between devices: 25.3 us -> 322 us  [connect_the_signs(): lax.all_to_all(jnp.stack([s0] * lax.axis_size(axis_tag)), axis_name=axis_...]
    all_gather x1, waiting for transfers between devices: 49.3 us -> 0.03 us  [on_device(): lax.all_gather(attn_out, ('grp', 'seq'), axis=1, tiled=True)]
    all_gather x1 -> x0, waiting for transfers between devices: 44.7 us -> none  [on_device(): lax.all_gather(attn_qkv, ('grp', 'seq'), axis=0, tiled=True)]
    all_to_all x0 -> x1, blocking collectives: none -> 16.9 us  [on_device(): lax.all_to_all(outgoing, 'seq', split_axis=0, concat_axis=0, tiled=True)]
    another operation x0 -> x1, local copies, waits for them, and re-layouts: none -> 5.88 us  [connect_the_signs(): jnp.stack([s0] * lax.axis_size(axis_tag))]
    all_to_all x1, waiting for transfers between devices: 13.7 us -> 7.95 us  [on_device(): lax.all_to_all(column_part, 'seq', split_axis=0, concat_axis=1, tiled=True)]
  transfers between devices with their start and end apart: 10 -> 9, of which waited for: 10 -> 8; matrix products, arithmetic and copies ran while one was open for 9% -> 4% of each run, Pallas kernels for 0% -> 0%
where the time goes in v1:
time: 554 us; the launch traced here: 552 us
  waiting for transfers between devices  427 us (77%)
  matrix products  49.8 us (9%)
  starting transfers between devices  22.1 us (4%)
  local copies, waits for them, and re-layouts  17.7 us (3%)
  blocking collectives  16.9 us (3%)
  between operations  15.1 us (3%)
    all_to_all x1, waiting for transfers between devices, connect_the_signs(): lax.all_to_all(jnp.stack([s0] * lax.axis_size(axis_tag)), axis_name=axis_...  322 us
    all_gather x1, waiting for transfers between devices, on_device(): lax.all_gather(merge_input, 'seq', axis=0, tiled=True)  44.6 us
    all_gather x1, waiting for transfers between devices, on_device(): lax.all_gather(hidden_part, 'seq', axis=1, tiled=True)  41.5 us
    all_to_all x1, blocking collectives, on_device(): lax.all_to_all(outgoing, 'seq', split_axis=0, concat_axis=0, tiled=True)  16.9 us
    ppermute x4, starting transfers between devices, from_behind(): lax.ppermute(value, axis, [(source, source + steps) for source in range(f...  14.4 us
  transfers between devices with their start and end apart: 9, of which 8 were waited for; matrix products, arithmetic and copies ran while one was open for 4% of the time, Pallas kernels for 0%

profile of v1, /device:TPU:0, one launch (start us, length us, event | category | flops | bytes accessed | tf_op | source)
XLA Modules:
  0.0 552.5 jit_solution(17661107504658586684)
XLA Ops:
  8.6 5.8 %convolution_convert_fusion.2 = bf16[64,3840]{1,0:T(8,128)(2,1)S(1)} fusion(bf16[1280,3840]{1,0:T(8,128)(2,1)} %param.22, bf16[64,1280]{1,0:T(8,128)(2,1)} %param.19, f32[1280]{0:T(1024)} %param.21, f32[64]{0:T(128)S(1)} %add_rsqrt_fusion.2), kind=kOutput, calls=%fused_computation.33 | convolution fusion | flops 629719040 | bytes 10491136 | tf_op jit(solution)/shard_map/while/body/eval_jaxpr/dot_general | solution.py:38
  15.2 2.0 reshape.352
  29.5 44.6 %all-gather.4.cloned.1.call-done = bf16[128,5120]{1,0:T(8,128)(2,1)} async-done(((bf16[16,5120]{1,0:T(8,128)(2,1)}), bf16[128,5120]{1,0:T(8,128)(2,1)}) %all-gather.4.cloned.1.call-update) | async-done | bytes 1310736 | tf_op jit(solution)/shard_map/all_gather | solution.py:116
  74.2 5.8 %fusion.41 = bf16[128,640]{1,0:T(8,128)(2,1)} fusion(bf16[128,5120]{1,0:T(8,128)(2,1)} %all-gather.4.cloned.1.call-done, bf16[5120,640]{1,0:T(8,128)(2,1)} %param.25), kind=kOutput, calls=%fused_computation.56 | convolution fusion | flops 844185600 | bytes 8028160 | tf_op jit(solution)/shard_map/dot_general | solution.py:115
  80.0 41.5 %all-gather.6.cloned.1.call-done = bf16[128,5120]{1,0:T(8,128)(2,1)} async-done(((bf16[128,640]{1,0:T(8,128)(2,1)}), bf16[128,5120]{1,0:T(8,128)(2,1)}) %all-gather.6.cloned.1.call-update) | async-done | bytes 1310736 | tf_op jit(solution)/shard_map/all_gather | solution.py:123
  121.5 6.6 %convolution_convert_fusion.3 = bf16[128,1024]{1,0:T(8,128)(2,1)} fusion(bf16[128,5120]{1,0:T(8,128)(2,1)} %all-gather.6.cloned.1.call-done, bf16[5120,1024]{1,0:T(8,128)(2,1)} %param.26), kind=kOutput, calls=%fused_computation.44 | convolution fusion | flops 1342308352 | bytes 12058624 | tf_op jit(solution)/shard_map/dot_general | solution.py:122
  128.1 3.5 all-to-all-start
  131.9 8.0 %all-to-all-done = bf16[8,16,1024]{2,1,0:T(8,128)(2,1)S(1)} async-done(((bf16[8,16,1024]{2,1,0:T(8,128)(2,1)}), bf16[8,16,1024]{2,1,0:T(8,128)(2,1)S(1)}, u32[]{:S(2)}, u32[]{:S(2)}) %all-to-all-start) | async-done | bytes 262176 | tf_op jit(solution)/shard_map/all_to_all | solution.py:131
  140.8 16.9 %all_to_all.29 = bf16[8,4,8192]{2,1,0:T(4,128)(2,1)S(1)} all-to-all(bf16[8,4,8192]{2,1,0:T(4,128)(2,1)S(1)} %copy.46), channel_id=1, replica_groups=mesh['grp'=4,'seq'=8] {'seq'}, dimensions={0} | all-to-all | bytes 1048576 | tf_op jit(solution)/shard_map/all_to_all | solution.py:139
  157.7 5.9 %stack.2 = bf16[32,256,768]{2,1,0:T(8,128)(2,1)} broadcast(bf16[256,768]{1,0:T(8,128)(2,1)S(1)} %copy-done.3), dimensions={1,2} | broadcast | bytes 12976128 | tf_op jit(solution)/shard_map/stack | solution.py:96
  163.6 3.9 all-to-all-start.2
  168.5 4.8 fusion.21
  173.3 322.1 %all-to-all-done.2 = bf16[32,256,768]{2,1,0:T(8,128)(2,1)} async-done(((bf16[32,256,768]{2,1,0:T(8,128)(2,1)}), bf16[32,256,768]{2,1,0:T(8,128)(2,1)}, u32[]{:S(2)}, u32[]{:S(2)}) %all-to-all-start.2) | async-done | bytes 12582944 | tf_op jit(solution)/shard_map/all_to_all | solution.py:95
  495.4 9.3 %fusion.28 = bf16[256,768]{1,0:T(8,128)(2,1)S(1)} fusion(bf16[8192,768]{1,0:T(8,128)(2,1)} %bitcast.6, bf16[256,8192]{1,0:T(8,128)(2,1)} %get-tuple-element.202, f32[8192]{0:T(1024)S(1)} %copy-done.6, f32[256]{0:T(256)S(1)} %add_rsqrt_fusion), kind=kOutput, calls=%fused_computation.38 | convolution fusion | flops 3229810688 | bytes 17204224 | tf_op jit(solution)/shard_map/dot_general | solution.py:148
  504.9 25.0 %while.20 = (s32[]{:T(128)}, bf16[256,256]{1,0:T(8,128)(2,1)S(1)}, bf16[1280,256]{1,0:T(8,128)(2,1)S(1)}, s32[]{:T(128)}, s32[]{:T(128)}, /*index=5*/s32[]{:T(128)}, s32[]{:T(128)}, s32[]{:T(128)}) while((s32[]{:T(128)}, bf16[256,256]{1,0:T(8,128)(2,1)S(1)}, bf16[1280,256]{1,0:T(8,128)(2,1)S(1)}, s32[]{:T(128)}, s32[]{:T(128)}, ...), condition=%wide.region_9.10_spmd, body=%wide.region_8.9_spmd.sunk | while | flops 7 | bytes 1048763 | solution.py:172
  506.2 2.9 collective-permute-done
  509.2 4.4 collective-permute-start
  513.6 2.5 collective-permute-done
  516.1 4.4 collective-permute-start
  520.5 2.5 collective-permute-done
  523.0 4.4 collective-permute-start
  527.4 2.5 collective-permute-done
  529.9 5.9 %while.21 = (s32[]{:T(128)}, bf16[4,256,128]{1,2,0:T(8,128)(2,1)S(1)}, s32[256]{0:T(256)S(1)}, bf16[4,256,128]{2,1,0:T(8,128)(2,1)S(1)}, bf16[1280,256]{1,0:T(8,...) while((s32[]{:T(128)}, bf16[4,256,128]{1,2,0:T(8,128)(2,1)S(1)}, s32[256]{0:T(256)S(1)}, ...), condition=%wide.region_13.14_spmd.clone, body=%wide.region_10.13_spmd.clone.sunk | while | flops 171115520 | bytes 5002349 | solution.py:187
  535.8 9.2 %fusion.19 = bf16[256,8192]{1,0:T(8,128)(2,1)} fusion(bf16[256,512]{0,1:T(8,128)(2,1)S(1)} %bitcast.74, bf16[512,8192]{1,0:T(8,128)(2,1)} %all-gather.8.cloned.1.call-done, bf16[256,8192]{1,0:T(8,128)(2,1)} %get-tuple-element.202), kind=kOutput, calls=%fused_computation.26 | convolution fusion | flops 2153775104 | bytes 17039360 | tf_op jit(solution)/shard_map/dot_general | solution.py:188
  (98 shorter events, 23.6 us)
Async XLA Ops:
  7.4 19.4 %copy-start = (bf16[1280,1280]{1,0:T(8,128)(2,1)S(1)}, bf16[1280,1280]{1,0:T(8,128)(2,1)}, u32[]{:S(2)}) copy-start(bf16[1280,1280]{1,0:T(8,128)(2,1)} %param.23) | copy-start | bytes 9830404
  7.4 66.8 %all-gather.4.cloned.1.call-start = ((), (), s32[]{:S(2)}) async-start(), calls=%async_computation.3 | async-start | bytes 1474560 | tf_op jit(solution)/shard_map/all_gather | solution.py:116
  8.6 12.6 %copy-start.5 = (s32[1,64]{1,0:T(1,128)S(1)}, s32[1,64]{1,0:T(1,128)}, u32[]{:S(2)}) copy-start(s32[1,64]{1,0:T(1,128)} %param.20) | copy-start | bytes 772
  14.4 12.4 %copy-start.2 = (bf16[64,1280]{1,0:T(8,128)(2,1)S(1)}, bf16[64,1280]{1,0:T(8,128)(2,1)}, u32[]{:S(2)}) copy-start(bf16[64,1280]{1,0:T(8,128)(2,1)} %param.19) | copy-start | bytes 491524
  22.6 5.9 %copy-start.4 = (f32[1280]{0:T(1024)S(1)}, f32[1280]{0:T(1024)}, u32[]{:S(2)}) copy-start(f32[1280]{0:T(1024)} %param.24) | copy-start | bytes 15364
  29.5 92.0 %all-gather.6.cloned.1.call-start = ((), (), s32[]{:S(2)}) async-start(), calls=%async_computation.4 | async-start | bytes 1474560 | tf_op jit(solution)/shard_map/all_gather | solution.py:123
  79.9 51.7 %copy-start.8 = (s32[16]{0:T(128)S(1)}, s32[16]{0:T(128)}, u32[]{:S(2)}) copy-start(s32[16]{0:T(128)} %param.27) | copy-start | bytes 196
  128.1 29.6 %copy-start.3 = (bf16[256,768]{1,0:T(8,128)(2,1)S(1)}, bf16[256,768]{1,0:T(8,128)(2,1)}, u32[]{:S(2)}) copy-start(bf16[256,768]{1,0:T(8,128)(2,1)} %param.32) | copy-start | bytes 1179652
  128.1 11.7 %all-to-all-start = ((bf16[8,16,1024]{2,1,0:T(8,128)(2,1)}), bf16[8,16,1024]{2,1,0:T(8,128)(2,1)S(1)}, u32[]{:S(2)}, u32[]{:S(2)}) async-start(bf16[8,16,1024]{2,1,0:T(8,128)(2,1)} %bitcast.3), calls=%async_computation | async-start | bytes 524288 | tf_op jit(solution)/shard_map/all_to_all | solution.py:131
  163.6 4.5 copy-start.9
  163.6 4.8 copy-start.7
  163.6 331.9 %all-to-all-start.2 = ((bf16[32,256,768]{2,1,0:T(8,128)(2,1)}), bf16[32,256,768]{2,1,0:T(8,128)(2,1)}, u32[]{:S(2)}, u32[]{:S(2)}) async-start(bf16[32,256,768]{2,1,0:T(8,128)(2,1)} %stack.2), calls=%async_computation.2 | async-start | bytes 25165824 | tf_op jit(solution)/shard_map/all_to_all | solution.py:95
  167.5 368.3 %all-gather.8.cloned.1.call-start = ((), (), s32[]{:S(2)}) async-start(), calls=%async_computation.5 | async-start | bytes 8650752 | tf_op jit(solution)/shard_map/all_gather | solution.py:190
  168.5 326.9 %copy-start.6 = (f32[8192]{0:T(1024)S(1)}, f32[8192]{0:T(1024)}, u32[]{:S(2)}) copy-start(f32[8192]{0:T(1024)} %param.31) | copy-start | bytes 98308
  504.9 4.2 collective-permute-start
  509.2 6.9 %collective-permute-start = (bf16[256,256]{1,0:T(8,128)(2,1)S(1)}, bf16[256,256]{1,0:T(8,128)(2,1)S(1)}, u32[]{:S(2)}, u32[]{:S(2)}) collective-permute-start(bf16[256,256]{1,0:T(8,128)(2,1)S(1)} %get-tuple-element.278), channel_id=1, source_target_pairs={{0,1},{1,2},{2,3},{3,4},{4,5},{5,6},{6,7},{8,9},{9,10},{10,11},{11... | collective-permute-start | bytes 393224 | tf_op jit(solution)/shard_map/while/body/eval_jaxpr/ppermute | solution.py:14
  516.1 6.9 %collective-permute-start = (bf16[256,256]{1,0:T(8,128)(2,1)S(1)}, bf16[256,256]{1,0:T(8,128)(2,1)S(1)}, u32[]{:S(2)}, u32[]{:S(2)}) collective-permute-start(bf16[256,256]{1,0:T(8,128)(2,1)S(1)} %get-tuple-element.278), channel_id=1, source_target_pairs={{0,1},{1,2},{2,3},{3,4},{4,5},{5,6},{6,7},{8,9},{9,10},{10,11},{11... | collective-permute-start | bytes 393224 | tf_op jit(solution)/shard_map/while/body/eval_jaxpr/ppermute | solution.py:14
  523.0 6.9 %collective-permute-start = (bf16[256,256]{1,0:T(8,128)(2,1)S(1)}, bf16[256,256]{1,0:T(8,128)(2,1)S(1)}, u32[]{:S(2)}, u32[]{:S(2)}) collective-permute-start(bf16[256,256]{1,0:T(8,128)(2,1)S(1)} %get-tuple-element.278), channel_id=1, source_target_pairs={{0,1},{1,2},{2,3},{3,4},{4,5},{5,6},{6,7},{8,9},{9,10},{10,11},{11... | collective-permute-start | bytes 393224 | tf_op jit(solution)/shard_map/while/body/eval_jaxpr/ppermute | solution.py:14
  535.8 9.2 %copy-start.1 = (bf16[1280,1280]{1,0:T(8,128)(2,1)S(1)}, bf16[1280,1280]{1,0:T(8,128)(2,1)}, u32[]{:S(2)}) copy-start(bf16[1280,1280]{1,0:T(8,128)(2,1)} %param.23) | copy-start | bytes 9830404
Sparse Core Ops, SparseCore 0:
  29.6 44.5 all-gather.3
  80.1 41.3 all-gather.5
Sparse Core Ops, SparseCore 1:
  170.8 276.9 all-gather.7
